TPU v7x, 32 devices: a whole 2x2x4 slice. The times are simulated.
32 devices in a mesh: band: 2 (over x), tm: 16 (over z, y, core).
Axes of the slice: x: 2, y: 2, z: 4, core: 2. Of those that a mesh axis runs over, the one named last changes fastest.
Arguments:
- voltages: bfloat16 [16, 2, 512, 4096], P('band', None, None, 'tm'), parts along dimension 0, may hold values from -12 to 12
- antenna_flags: int32 [32, 16], P('tm', 'band'), parts along dimension 1, may hold values from -2147483648 to 2147483647, as said below
- owned_tile: int32 [16], replicated, may hold values from 0 to 15, each once
Outputs:
- visibility: float32 [512, 16, 2, 512], P('tm', 'band'), parts along dimension 1
There are 2 independent parts, one for each index of `band`. A program takes and returns all parts, laid end to end along the dimension named above; an argument that names none is the same for every part. Nothing has to cross between parts.
Inputs may be any that keep to these rules, and one draw needn't show every extreme that they name: `antenna_flags`: bit b of word w of sub-integration s is 1 where the samples of both polarisations of antenna 32 * w + b are good in that sub-integration of 128 samples, 0 where flagged; all 32 bits of a word are used; some antennas may be flagged in every sub-integration. A permutation: the index k of tm holds the baseline rows of tile owned_tile[k].
All inputs are finite; a program needn't handle non-finite values.
Results may differ from a plain program's by a relative error of at most 0.0003.
Values sent between devices are 32-bit elements; how exact they have to be, the bound alone decides.
A program may use at most 128 MiB of HBM per device.

v0:
```python
import jax
import jax.numpy as jnp
from jax import lax
from jax.sharding import PartitionSpec as P


def unpack_flags(words):
    shifts = jnp.arange(32, dtype=jnp.int32)
    bits = jnp.bitwise_and(jnp.right_shift(words[:, :, None], shifts[None, None, :]), 1)
    return bits.reshape(words.shape[0], words.shape[1] * 32)


def stack_operands(masked):
    real_part = masked[:, 0]
    imag_part = masked[:, 1]
    right_side = jnp.concatenate([real_part, imag_part], axis=-1)
    left_side = jnp.stack([right_side, jnp.concatenate([imag_part, -real_part], axis=-1)], axis=1)
    return (left_side, right_side)


def shards(voltages, antenna_flags, owned_tile):
    axis_count = lax.axis_size("tm")
    my_index = lax.axis_index("tm")
    inputs = voltages.shape[2]
    samples = voltages.shape[3]
    block_rows = inputs // axis_count
    sub_length = samples // antenna_flags.shape[0]
    every_word = lax.all_gather(antenna_flags, "tm", axis=0, tiled=True)
    every_flag = unpack_flags(every_word)
    local_flag = unpack_flags(antenna_flags)
    own_tile = owned_tile[my_index]
    own_antennas = (own_tile * block_rows + jnp.arange(block_rows, dtype=jnp.int32)) // 2
    own_flags = jnp.take(every_flag, own_antennas, axis=1)
    input_flags = jnp.repeat(every_flag, 2, axis=1)
    counts = sub_length * jnp.dot(own_flags.T, input_flags)
    divisor = jnp.maximum(counts, 1).astype(jnp.float32)[:, None, None, :]
    sample_flags = jnp.repeat(jnp.repeat(local_flag, 2, axis=1).T, sub_length, axis=1).astype(
        jnp.bfloat16
    )
    masked = voltages * sample_flags[None, None]
    left_side, right_side = stack_operands(masked)
    row_index = (
        owned_tile[:, None] * block_rows + jnp.arange(block_rows, dtype=jnp.int32)[None, :]
    ).reshape(-1)
    picked = jnp.take(left_side, row_index, axis=2)
    summed = lax.psum_scatter(
        jnp.einsum("ckru,cju->rckj", picked, right_side, preferred_element_type=jnp.float32),
        "tm",
        scatter_dimension=0,
        tiled=True,
    )
    return summed / divisor


def solution(mesh):
    return jax.shard_map(
        shards,
        mesh=mesh,
        in_specs=(P("band", None, None, "tm"), P("tm", "band"), P()),
        out_specs=P("tm", "band", None, None),
        check_vma=False,
    )
```

profile of v0, /device:TPU:0, one launch (start us, length us, event | category | flops | bytes accessed | tf_op | source)
XLA Modules:
  0.0 301.0 jit_solution(14204660816384712198)
XLA Ops:
  6.5 0.0 reduce-scatter.2.cloned.1.call-start
  6.5 0.1 shift_right_arithmetic.43
  6.6 0.8 copy.18
  7.4 0.1 fusion.7
  7.5 0.1 broadcast_in_dim.37
  7.6 0.6 broadcast_in_dim.38
  8.2 2.7 copy_multiply_fusion
  10.9 0.0 copy-start.1
  10.9 1.7 slice_bitcast_fusion.1
  12.5 1.5 fusion.14
  14.0 0.1 iota_add_fusion
  14.1 0.1 add.111
  14.2 0.1 add.108
  14.2 6.3 %fusion.2 = (bf16[8,1,512,512]{3,2,0,1:T(8,128)(2,1)}, bf16[8,1,512,512]{3,2,0,1:T(8,128)(2,1)}) fusion(bf16[8,512,256]{2,1,0:T(8,128)(2,1)} %get-tuple-element.6, bf16[8,512,256]{2,1,0:T(8,128)(2,1)S(1)} %get-tuple-element.5, bf16[8,512,256]{2,1,0:T(8,128)(2,1)} %fusion.14), kind=kLoop, calls=%fused_computation.10 | loop fusion | flops 16777216 | bytes 14680064 | tf_op jit(solution)/shard_map/stack | solution.py:17
  20.6 7.4 %pad_maximum_fusion = bf16[8,2,512,512]{3,2,0,1:T(8,128)(2,1)} fusion(bf16[8,1,512,512]{3,2,0,1:T(8,128)(2,1)} %get-tuple-element.8, bf16[8,1,512,512]{3,2,0,1:T(8,128)(2,1)} %get-tuple-element.7), kind=kLoop, calls=%fused_computation.3 | loop fusion | flops 4194304 | bytes 16777216 | tf_op jit(solution)/shard_map/stack | solution.py:17
  28.0 11.3 %copy.20 = bf16[8,2,512,512]{3,0,2,1:T(8,128)(2,1)} copy(bf16[8,2,512,512]{3,2,0,1:T(8,128)(2,1)} %pad_maximum_fusion) | data formatting | bytes 16777216 | tf_op jit(solution)/shard_map/stack | solution.py:17
  39.4 23.2 %gather_fusion = bf16[512,8,2,512]{3,1,2,0:T(8,128)(2,1)} fusion(bf16[8,2,512,512]{3,0,2,1:T(8,128)(2,1)} %copy.20, s32[1024]{0:T(1024)S(1)} %pad_clamp_fusion.1), kind=kCustom, calls=%fused_computation | custom fusion | bytes 16779264 | tf_op jit(solution)/shard_map/jit(_take)/gather | solution.py:45
  62.6 7.6 %select_bitcast_fusion = bf16[8,2,512,512]{3,0,1,2:T(8,128)(2,1)} fusion(bf16[512,8,2,512]{3,1,2,0:T(8,128)(2,1)} %gather_fusion, pred[512]{0:T(512)(128)(4,1)S(1)} %compare_and_fusion.1), kind=kLoop, calls=%fused_computation.5 | loop fusion | flops 4194304 | bytes 16777728 | tf_op jit(solution)/shard_map/jit(_take)/select_n | solution.py:45
  70.2 20.3 %convolution_bitcast_fusion = f32[512,8,2,512]{0,3,2,1:T(8,128)} fusion(bf16[8,2,512,512]{3,0,1,2:T(8,128)(2,1)} %select_bitcast_fusion, bf16[8,512,256]{2,1,0:T(8,128)(2,1)} %get-tuple-element.6, bf16[8,512,256]{2,1,0:T(8,128)(2,1)S(1)} %get-tuple-element.5), kind=kOutput, calls=%fused_computation.2 | convolution fusion | flops 4303355904 | bytes 29360128 | tf_op jit(solution)/shard_map/ckru,cju->rckj/dot_general | solution.py:47
  90.6 20.2 %copy.22 = f32[512,8,2,512]{3,1,2,0:T(8,128)} copy(f32[512,8,2,512]{0,3,2,1:T(8,128)} %convolution_bitcast_fusion) | data formatting | bytes 33554432 | tf_op jit(solution)/shard_map/ckru,cju->rckj/transpose | solution.py:47
  110.8 0.0 reduce-scatter.2.cloned.1.call-update
  110.8 0.6 dynamic_slice.3
  111.4 0.1 copy-done
  111.5 23.1 %all-gather = s32[16,2,8]{2,1,0:T(2,128)S(1)} all-gather(s32[1,2,8]{2,1,0:T(2,128)S(1)} %bitcast.50), channel_id=1, replica_groups=mesh['band'=2,'tm'=16] {'tm'}, dimensions={0}, use_global_device_ids=true | all-gather | bytes 1088 | tf_op jit(solution)/shard_map/all_gather | solution.py:28
  134.6 0.1 copy.23
  134.7 0.1 fusion.5
  135.5 0.6 gather_fusion.1
  136.1 0.1 broadcast_in_dim.43
  136.2 0.6 fusion.4
  136.7 154.3 %reduce-scatter.2.cloned.1.call-done = f32[32,8,2,512]{3,1,2,0:T(8,128)} async-done(((f32[512,8,2,512]{3,1,2,0:T(8,128)}), f32[32,8,2,512]{3,1,2,0:T(8,128)}) %reduce-scatter.2.cloned.1.call-update) | async-done | bytes 1048592 | tf_op jit(solution)/shard_map/reduce_scatter | solution.py:46
  291.0 1.4 broadcast_divide_fusion
  292.4 1.8 copy.24
  (11 shorter events, 0.1 us)
Async XLA Ops:
  6.5 284.5 %reduce-scatter.2.cloned.1.call-start = ((), (), s32[]{:S(2)}) async-start(), calls=%async_computation.1 | async-start | bytes 17825792 | tf_op jit(solution)/shard_map/reduce_scatter | solution.py:46
  10.9 3.1 %copy-start.1 = (s32[16]{0:T(128)S(1)}, s32[16]{0:T(128)}, u32[]{:S(2)}) copy-start(s32[16]{0:T(128)} %param.5) | copy-start | bytes 196
  110.8 0.7 copy-start
Sparse Core Ops, SparseCore 0:
  110.9 180.0 reduce-scatter.1
where the time goes:
time: 302 us; the launch traced here: 301 us
  waiting for transfers between devices  154 us (51%)
  local copies, waits for them, and re-layouts  61.3 us (20%)
  other arithmetic  27.2 us (9%)
  blocking collectives  23.1 us (8%)
  matrix products  20.9 us (7%)
  between operations  14.2 us (5%)
    reduce_scatter x1, waiting for transfers between devices, shards(): lax.psum_scatter(jnp.einsum('ckru,cju->rckj', picked, right_side, preferr...  154 us
    gather x1, local copies, waits for them, and re-layouts, shards(): picked = jnp.take(left_side, row_index, axis=2)  23.2 us
    all_gather x1, blocking collectives, shards(): every_word = lax.all_gather(antenna_flags, 'tm', axis=0, tiled=True)  23.1 us
    dot_general x1, matrix products, shards(): jnp.einsum('ckru,cju->rckj', picked, right_side, preferred_element_type=j...  20.3 us
    transpose x1, local copies, waits for them, and re-layouts, shards(): jnp.einsum('ckru,cju->rckj', picked, right_side, preferred_element_type=j...  20.2 us
    another operation x2, other arithmetic, stack_operands(): jnp.stack([right_side, jnp.concatenate([imag_part, -real_part], axis=-1)]...  13.8 us
    another operation x1, local copies, waits for them, and re-layouts, stack_operands(): jnp.stack([right_side, jnp.concatenate([imag_part, -real_part], axis=-1)]...  11.3 us
    select_n x2, other arithmetic, shards(): picked = jnp.take(left_side, row_index, axis=2)  7.63 us
  transfers between devices with their start and end apart: 1, of which 1 were waited for; matrix products, arithmetic and copies ran while one was open for 1% of the time, Pallas kernels for 0%

commit v1 on v0

v1 whole, which is shorter than its diff:
```python
import functools

import jax
import jax.numpy as jnp
from jax import lax
from jax.experimental import pallas as pl
from jax.experimental.pallas import tpu as pltpu
from jax.sharding import PartitionSpec as P

MESH = pl.DeviceIdType.MESH
CORES = 2


def grid_of(mesh):
    count = mesh.shape["tm"]
    ny = 2 if mesh.shape["band"] < 4 and count % (4 * CORES) == 0 else 1
    return count // (ny * CORES), ny


def rank_of(index, nz, ny):
    return ((index % CORES) * ny + (index // CORES) % ny) * nz + index // (CORES * ny)


def kernel(nz, ny, first, owned, flags, volts, summed, mirrored, mask, plane, gram, from_core,
           from_y, from_z, turned, cs, cr, ys, yr, zs, zr, fs, fr):
    count = nz * ny * CORES
    chans, _, tiles, rows, samples = volts.shape
    inputs = tiles * rows
    me = lax.axis_index("tm")
    core = lax.rem(me, CORES)
    y = lax.rem(me // CORES, ny)
    z = me // (CORES * ny)

    def index_at(zz, yy, cc):
        return (zz * ny + yy) * CORES + cc

    barrier = pltpu.get_barrier_semaphore()

    def greet(step, carry):
        pl.semaphore_signal(
            barrier, inc=1, device_id={"tm": lax.rem(me + step, count)}, device_id_type=MESH
        )
        return carry

    lax.fori_loop(1, count, greet, 0)

    subs, words = flags.shape
    length = samples // subs
    span = inputs // words
    shift = lax.broadcasted_iota(jnp.int32, (span, length), 0) // 2
    for word in range(words):
        for sub in range(subs):
            bits = jnp.right_shift(jnp.full((span, length), flags[sub, word], jnp.int32), shift)
            good = jnp.bitwise_and(bits, 1).astype(jnp.float32).astype(mask.dtype)
            good = good.reshape(span // rows, rows, length)
            mask[word * (span // rows) : (word + 1) * (span // rows), :, sub * length : (sub + 1) * length] = good
    pl.semaphore_wait(barrier, count - 1)

    def remote(src, dst, send, recv, target):
        return pltpu.make_async_remote_copy(
            src_ref=src, dst_ref=dst, send_sem=send, recv_sem=recv,
            device_id={"tm": target}, device_id_type=MESH,
        )

    def core_copy(ch):
        return remote(gram.at[ch, 1 - core], from_core.at[ch], cs.at[ch], cr.at[ch], index_at(z, y, 1 - core))

    def y_copy(ch):
        if ny == 1:
            return None
        return remote(gram.at[ch, core, 1 - y], from_y.at[ch], ys.at[ch], yr.at[ch], index_at(z, 1 - y, core))

    def y_last_copy(ch):
        return remote(from_z.at[ch, nz - 2, 1 - y], from_y.at[ch, 0], ys.at[ch], yr.at[ch], index_at(z, 1 - y, core))

    def z_way(ch):
        return 1 - 2 * (ch % 2)

    def z_copy(ch, step, wide):
        way = z_way(ch)
        target = index_at(lax.rem(z + way + nz, nz), y, core)
        dest = lax.rem(z - way * (1 + step) + nz * 2, nz)
        if step == 0:
            src = gram.at[ch, core, :, dest] if wide else gram.at[ch, core, y, dest]
        else:
            src = from_z.at[ch, step - 1] if wide else from_z.at[ch, step - 1, 0]
        dst = from_z.at[ch, step] if wide else from_z.at[ch, step, 0]
        return remote(src, dst, zs.at[ch, step], zr.at[ch, step], target)

    def compute(ch):
        for tile in range(count):
            c, rest = divmod(tile, ny * nz)
            yy, zz = divmod(rest, nz)
            source = owned[index_at(zz, yy, c)]
            good = mask[source]
            for part in range(2):
                value = volts[ch, part, source].astype(mask.dtype) * good
                plane[tile * rows : (tile + 1) * rows, part * samples : (part + 1) * samples] = value
        half = inputs // CORES
        pair = plane[...].astype(jnp.bfloat16)
        for turn in range(CORES):
            c = (core + 1 + turn) % CORES
            part = plane[pl.ds(pl.multiple_of(c * half, half), half), :].astype(jnp.bfloat16)
            other = jnp.concatenate([part[:, samples:], -part[:, :samples]], axis=1)
            dims = (((1,), (1,)), ((), ()))
            total = lax.dot_general(part, pair, dims, preferred_element_type=jnp.float32)
            total += lax.dot_general(other, pair, dims, preferred_element_type=jnp.float32)
            gram[ch, c] = total.reshape(ny, nz, rows, inputs)
            if turn == 0:
                core_copy(ch).start()

    def after_core(ch):
        core_copy(ch).wait()
        gram[ch, core] += from_core[ch]

    def begin(ch):
        after_core(ch)
        if ny == 1:
            z_copy(ch, 0, False).start()
            return

        @pl.when(ch < first)
        def _():
            z_copy(ch, 0, True).start()

        @pl.when(ch >= first)
        def _():
            y_copy(ch).start()

    def body(ch, carry):
        compute(ch)

        @pl.when(ch > 0)
        def _():
            begin(ch - 1)

        return carry

    lax.fori_loop(0, chans, body, 0)
    begin(chans - 1)

    def after_z(ch, step, wide):
        z_copy(ch, step, wide).wait()
        way = z_way(ch)
        dest = lax.rem(z - way * (2 + step) + nz * 2, nz)
        if wide:
            from_z[ch, step] += gram[ch, core, :, dest]
        else:
            value = from_z[ch, step, 0] + gram[ch, core, y, dest]
            if step == nz - 2:
                summed[ch] = value
            else:
                from_z[ch, step, 0] = value
        if step < nz - 2:
            z_copy(ch, step + 1, wide).start()
        elif wide:
            y_last_copy(ch).start()

    def after_y(ch):
        y_copy(ch).wait()
        gram[ch, core, y] += from_y[ch]
        z_copy(ch, 0, False).start()

    def after_last_y(ch):
        y_last_copy(ch).wait()
        summed[ch] = from_z[ch, nz - 2, y] + from_y[ch, 0]

    events = []
    for ch in range(chans):
        if ny == 1:
            for step in range(nz - 1):
                events.append((step * chans + ch, after_z, (ch, step, False)))
        elif ch < first:
            for step in range(nz - 1):
                events.append((8.0 * (step + 1), after_z, (ch, step, True)))
            events.append((8.0 * nz, after_last_y, (ch,)))
        else:
            start = 5.8 * (ch - first + 1)
            events.append((start, after_y, (ch,)))
            for step in range(nz - 1):
                events.append((start + 4.6 * (step + 1), after_z, (ch, step, False)))
    for _, act, args in sorted(events, key=lambda event: event[0]):
        act(*args)

    turned[...] = summed[...].reshape(chans * rows, inputs).T.reshape(count, rows, chans * rows)
    mine = rank_of(me, nz, ny)

    def block_copy(step):
        target = lax.rem(me + step, count)
        return remote(turned.at[rank_of(target, nz, ny)], mirrored.at[mine], fs.at[step], fr.at[step], target)

    def send(step, carry):
        block_copy(step).start()
        return carry

    def finish(step, carry):
        block_copy(step).wait()
        return carry

    lax.fori_loop(1, count, send, 0)
    mirrored[mine] = turned[mine]
    lax.fori_loop(1, count, finish, 0)


def shards(nz, ny, voltages, antenna_flags, owned_tile):
    count = nz * ny * CORES
    me = lax.axis_index("tm")
    chans, _, inputs, samples = voltages.shape
    rows = inputs // count
    sub_length = samples // antenna_flags.shape[0]
    first = chans // 4 if ny > 1 else 0
    held = jnp.bfloat16 if rows % 16 == 0 else jnp.float32
    vmem = pl.BlockSpec(memory_space=pltpu.VMEM)
    smem = pl.BlockSpec(memory_space=pltpu.SMEM)
    dma = pltpu.SemaphoreType.DMA
    summed, mirrored = pl.pallas_call(
        functools.partial(kernel, nz, ny, first),
        out_shape=(
            jax.ShapeDtypeStruct((chans, rows, inputs), jnp.float32),
            jax.ShapeDtypeStruct((count, rows, chans * rows), jnp.float32),
        ),
        in_specs=[smem, smem, vmem],
        out_specs=(vmem, vmem),
        scratch_shapes=[
            pltpu.VMEM((count, rows, samples), held),
            pltpu.VMEM((inputs, 2 * samples), held),
            pltpu.VMEM((chans, CORES, ny, nz, rows, inputs), jnp.float32),
            pltpu.VMEM((chans, ny, nz, rows, inputs), jnp.float32),
            pltpu.VMEM((chans, nz, rows, inputs), jnp.float32),
            pltpu.VMEM((chans, nz - 1, ny, rows, inputs), jnp.float32),
            pltpu.VMEM((count, rows, chans * rows), jnp.float32),
            dma((chans,)), dma((chans,)), dma((chans,)), dma((chans,)),
            dma((chans, nz - 1)), dma((chans, nz - 1)), dma((count,)), dma((count,)),
        ],
        compiler_params=pltpu.CompilerParams(
            collective_id=0, has_side_effects=True, vmem_limit_bytes=60 * 1024 * 1024
        ),
    )(owned_tile, antenna_flags, voltages.reshape(chans, 2, count, rows, samples))

    words = lax.all_gather(antenna_flags, "tm", axis=0, tiled=True)
    shifts = jnp.arange(32, dtype=jnp.int32)
    bits = jnp.bitwise_and(jnp.right_shift(words[:, :, None], shifts), 1)
    good = jnp.broadcast_to(bits[..., None], bits.shape + (2,)).reshape(words.shape[0], count, rows)
    good = good.astype(jnp.bfloat16)
    own = lax.dynamic_index_in_dim(good, owned_tile[me], 1, False)
    counts = jnp.einsum("su,stj->utj", own, good, preferred_element_type=jnp.float32)
    scale = 0.5 / jnp.maximum(sub_length * counts, 1.0)

    holder = jnp.zeros((count,), jnp.int32).at[owned_tile].set(
        rank_of(jnp.arange(count, dtype=jnp.int32), nz, ny)
    )
    direct = summed.reshape(chans, rows, count, rows)[:, :, holder].transpose(1, 0, 2, 3)
    mirror = mirrored.reshape(count, rows, chans, rows)[holder].transpose(1, 2, 0, 3)
    scale = scale[:, None]
    real = ((direct + mirror) * scale).reshape(rows, chans, inputs)
    imag = ((direct - mirror) * scale).reshape(rows, chans, inputs)
    return jnp.stack([real, imag], axis=2)


def solution(mesh):
    nz, ny = grid_of(mesh)
    return jax.shard_map(
        functools.partial(shards, nz, ny),
        mesh=mesh,
        in_specs=(P("band", None, None, "tm"), P("tm", "band"), P()),
        out_specs=P("tm", "band", None, None),
        check_vma=False,
    )
```

time: 302 us -> 126 us (0.42)
  waiting for transfers between devices: 154 us -> 0 us
  Pallas kernels: 0 us -> 76.7 us
  local copies, waits for them, and re-layouts: 61.3 us -> 18.5 us
  other arithmetic: 27.2 us -> 4.58 us
  matrix products: 20.9 us -> 0.32 us
  between operations: 14.2 us -> 2.06 us
    reduce_scatter x1 -> x0, waiting for transfers between devices: 154 us -> none  [shards(): lax.psum_scatter(jnp.einsum('ckru,cju->rckj', picked, right_side, preferr...]
    pallas_call x0 -> x1, Pallas kernels: none -> 76.7 us  [shards(): pl.pallas_call(functools.partial(kernel, nz, ny, first), out_shape=(jax.S...]
    dot_general x2 -> x1, matrix products: 20.9 us -> 0.32 us  [shards(): jnp.einsum('su,stj->utj', own, good, preferred_element_type=jnp.float32)]
    transpose x1 -> x0, local copies, waits for them, and re-layouts: 20.2 us -> none  [shards(): jnp.einsum('ckru,cju->rckj', picked, right_side, preferred_element_type=j...]
    gather x2, local copies, waits for them, and re-layouts: 23.8 us -> 5.64 us  [the longest x1 3.66 us: shards(): summed.reshape(chans, rows, count, rows)[:, :, holder].transpose(1, 0, 2, 3)]
    another operation x2 -> x1, other arithmetic: 13.8 us -> 0.07 us  [shards(): return jnp.stack([real, imag], axis=2)]
    another operation x1 -> x3, local copies, waits for them, and re-layouts: 11.3 us -> 3.44 us  [shards(): return jnp.stack([real, imag], axis=2)]
    select_n x3 -> x2, other arithmetic: 7.64 us -> 0.01 us  [the longest x1 0.01 us: shards(): jnp.zeros((count,), jnp.int32).at[owned_tile]]
  transfers between devices with their start and end apart: 1 -> 0, of which waited for: 1 -> 0; matrix products, arithmetic and copies ran while one was open for 1% -> 0% of each run, Pallas kernels for 0% -> 0%
where the time goes in v1:
time: 126 us; the launch traced here: 125 us
  Pallas kernels  76.7 us (61%)
  blocking collectives  23.2 us (18%)
  local copies, waits for them, and re-layouts  18.5 us (15%)
  other arithmetic  4.58 us (4%)
  between operations  2.06 us (2%)
    pallas_call x1, Pallas kernels, shards(): pl.pallas_call(functools.partial(kernel, nz, ny, first), out_shape=(jax.S...  76.7 us
    all_gather x1, blocking collectives, shards(): words = lax.all_gather(antenna_flags, 'tm', axis=0, tiled=True)  23.2 us
    mul x1, other arithmetic, shards(): real = ((direct + mirror) * scale).reshape(rows, chans, inputs)  4.47 us
    gather x1, local copies, waits for them, and re-layouts, shards(): summed.reshape(chans, rows, count, rows)[:, :, holder].transpose(1, 0, 2, 3)  3.66 us
    reshape x2, local copies, waits for them, and re-layouts, shards(): summed.reshape(chans, rows, count, rows)[:, :, holder].transpose(1, 0, 2, 3)  3.58 us
    another operation x3, local copies, waits for them, and re-layouts, shards(): return jnp.stack([real, imag], axis=2)  3.44 us
    mul x1, local copies, waits for them, and re-layouts, shards(): real = ((direct + mirror) * scale).reshape(rows, chans, inputs)  2.81 us

profile of v1, /device:TPU:0, one launch (start us, length us, event | category | flops | bytes accessed | tf_op | source)
XLA Modules:
  0.0 125.3 jit_solution(17090329668740031175)
XLA Ops:
  0.0 76.7 %shard_map.37 = (f32[8,32,512]{2,1,0:T(8,128)}, f32[16,32,256]{2,1,0:T(8,128)}) custom-call(s32[16]{0:T(128)} %owned.1, s32[2,8]{1,0:T(2,128)} %flags.1, bf16[8,2,16,32,256]{4,3,2,1,0:T(8,128)(2,1)} %bitcast.24), custom_call_target="tpu_custom_call" | custom-call | tf_op jit(solution)/shard_map/pallas_call | solution.py:216
  76.7 1.6 %reshape.19 = f32[8,32,16,32]{3,2,1,0:T(8,128)S(1)} reshape(f32[8,32,512]{2,1,0:T(8,128)} %get-tuple-element.7) | data formatting | bytes 1048576 | tf_op jit(solution)/shard_map/reshape | solution.py:252
  78.3 0.0 copy-start.2
  78.3 1.9 %copy.20 = f32[8,32,16,32]{3,1,2,0:T(8,128)} copy(f32[8,32,16,32]{3,2,1,0:T(8,128)S(1)} %reshape.19) | data formatting | bytes 1048576 | tf_op jit(solution)/shard_map/reshape | solution.py:252
  80.3 0.0 copy-done.2
  80.3 0.6 scatter_custom_fusion
  80.9 0.0 copy-start
  80.9 3.7 %gather_fusion = f32[16,8,32,32]{3,2,1,0:T(8,128)} fusion(f32[8,32,16,32]{3,1,2,0:T(8,128)} %copy.20, s32[1024]{0:T(1024)S(1)} %pad_clamp_fusion), kind=kCustom, calls=%fused_computation | custom fusion | bytes 1048640 | tf_op jit(solution)/shard_map/gather | solution.py:252
  84.6 0.0 copy-done
  84.6 0.5 reshape.20
  85.1 0.0 copy-start.1
  85.1 2.0 %gather_fusion.1 = f32[16,32,8,32]{3,2,1,0:T(8,128)} fusion(f32[16,32,8,32]{3,2,1,0:T(8,128)S(1)} %reshape.20, s32[1024]{0:T(1024)S(1)} %pad_clamp_fusion), kind=kCustom, calls=%fused_computation.1 | custom fusion | bytes 1048640 | tf_op jit(solution)/shard_map/gather | solution.py:253
  87.1 0.0 copy-done.1
  87.1 23.2 %all-gather = s32[16,2,8]{2,1,0:T(2,128)S(1)} all-gather(s32[1,2,8]{2,1,0:T(2,128)S(1)} %bitcast.27), channel_id=1, replica_groups=mesh['band'=2,'tm'=16] {'tm'}, dimensions={0}, use_global_device_ids=true | all-gather | bytes 1088 | tf_op jit(solution)/shard_map/all_gather | solution.py:240
  110.3 0.1 copy.22
  110.4 0.1 broadcast_in_dim.8
  110.5 0.6 dynamic_slice.7
  113.0 0.3 fusion.3
  113.3 4.5 %fusion = (f32[32,8,16,32]{3,0,1,2:T(8,128)}, f32[32,8,16,32]{3,0,1,2:T(8,128)S(1)}) fusion(f32[16,8,32,32]{3,2,1,0:T(8,128)} %gather_fusion, f32[16,32,8,32]{3,2,1,0:T(8,128)} %gather_fusion.1, f32[32,16,32]{2,0,1:T(8,128)S(1)} %fusion.3), kind=kLoop, calls=%fused_computation.5 | loop fusion | flops 524288 | bytes 2162688 | tf_op jit(solution)/shard_map/mul | solution.py:255
  117.8 1.2 copy.25
  119.0 0.8 stack_reshape.7
  119.8 2.8 %copy.24 = f32[32,8,16,32]{3,2,1,0:T(8,128)S(1)} copy(f32[32,8,16,32]{3,0,1,2:T(8,128)} %get-tuple-element.9) | data formatting | bytes 1048576 | tf_op jit(solution)/shard_map/mul | solution.py:255
  122.7 0.8 stack_reshape.6
  123.5 0.1 pad_maximum_fusion
  123.6 1.8 %copy.26 = f32[32,8,2,512]{3,2,1,0:T(2,128)} copy(f32[32,8,2,512]{3,1,0,2:T(8,128)S(1)} %pad_maximum_fusion) | data formatting | bytes 2097152 | tf_op jit(solution)/shard_map/stack | solution.py:257
  (4 shorter events, 0.0 us)
Async XLA Ops:
  78.3 2.0 %copy-start.2 = (s32[16]{0:T(128)S(1)}, s32[16]{0:T(128)}, u32[]{:S(2)}) copy-start(s32[16]{0:T(128)} %owned.1) | copy-start | bytes 196
  80.9 3.7 %copy-start = (f32[16,32,256]{2,1,0:T(8,128)S(1)}, f32[16,32,256]{2,1,0:T(8,128)}, u32[]{:S(2)}) copy-start(f32[16,32,256]{2,1,0:T(8,128)} %get-tuple-element.8) | copy-start | bytes 1572868
  85.1 2.0 %copy-start.1 = (s32[2,8]{1,0:T(2,128)S(1)}, s32[2,8]{1,0:T(2,128)}, u32[]{:S(2)}) copy-start(s32[2,8]{1,0:T(2,128)} %flags.1) | copy-start | bytes 196

commit v2 on v1

--- a/solution.py
+++ b/solution.py
@@ -21,8 +21,9 @@
     return ((index % CORES) * ny + (index // CORES) % ny) * nz + index // (CORES * ny)
 
 
-def kernel(nz, ny, first, owned, flags, volts, summed, mirrored, mask, plane, gram, from_core,
-           from_y, from_z, turned, cs, cr, ys, yr, zs, zr, fs, fr):
+def kernel(nz, ny, first, owned, flags, packed, volts, kept, mirrored, words_all, mask, plane,
+           gram, from_core, from_y, from_z, summed, turned, gathered,
+           cs, cr, ys, yr, zs, zr, fs, fr, gs, gr):
     count = nz * ny * CORES
     chans, _, tiles, rows, samples = volts.shape
     inputs = tiles * rows
@@ -61,6 +62,13 @@
             src_ref=src, dst_ref=dst, send_sem=send, recv_sem=recv,
             device_id={"tm": target}, device_id_type=MESH,
         )
+
+    def flag_copy(step):
+        target = lax.rem(me + step, count)
+        return remote(packed, gathered.at[me], gs.at[step], gr.at[step], target)
+
+    for step in range(1, count):
+        flag_copy(step).start()
 
     def core_copy(ch):
         return remote(gram.at[ch, 1 - core], from_core.at[ch], cs.at[ch], cr.at[ch], index_at(z, y, 1 - core))
@@ -139,6 +147,12 @@
     lax.fori_loop(0, chans, body, 0)
     begin(chans - 1)
 
+    for step in range(1, count):
+        flag_copy(step).wait()
+    for index in range(count):
+        value = jnp.where(me == index, packed[...], gathered[index])
+        words_all[index * subs : (index + 1) * subs, :] = value[:subs, :words]
+
     def after_z(ch, step, wide):
         z_copy(ch, step, wide).wait()
         way = z_way(ch)
@@ -182,45 +196,91 @@
     for _, act, args in sorted(events, key=lambda event: event[0]):
         act(*args)
 
-    turned[...] = summed[...].reshape(chans * rows, inputs).T.reshape(count, rows, chans * rows)
+    flipped = summed[...].reshape(chans * rows, inputs).T.reshape(count, rows, chans * rows)
+    turned[...] = flipped
+    kept[...] = flipped
     mine = rank_of(me, nz, ny)
 
     def block_copy(step):
         target = lax.rem(me + step, count)
         return remote(turned.at[rank_of(target, nz, ny)], mirrored.at[mine], fs.at[step], fr.at[step], target)
 
-    def send(step, carry):
+    for step in range(1, count):
         block_copy(step).start()
-        return carry
-
-    def finish(step, carry):
+    for step in range(1, count):
         block_copy(step).wait()
-        return carry
-
-    lax.fori_loop(1, count, send, 0)
     mirrored[mine] = turned[mine]
-    lax.fori_loop(1, count, finish, 0)
+
+
+def assemble(nz, ny, length, owned, words_all, kept, mirrored, out, pairs, holder):
+    count, rows, width = kept.shape
+    slots, words = words_all.shape
+    inputs = count * rows
+    chans = width // rows
+    span = inputs // words
+    me = lax.axis_index("tm")
+    every = words_all[...]
+    width = max(span, 128)
+    lane = lax.broadcasted_iota(jnp.int32, (slots, width), 1)
+    columns = []
+    for word in range(0, words, width // span):
+        value = jnp.broadcast_to(every[:, word : word + 1], (slots, width))
+        for extra in range(1, width // span):
+            value = jnp.where(lane >= extra * span, every[:, word + extra : word + extra + 1], value)
+        bits = jnp.right_shift(value, (lane % span) // 2)
+        columns.append(jnp.bitwise_and(bits, 1).astype(jnp.float32))
+    good = jnp.concatenate(columns, axis=1).astype(jnp.bfloat16)
+    counts = lax.dot_general(good, good, (((0,), (0,)), ((), ())), preferred_element_type=jnp.float32)
+    pairs[...] = counts.reshape(count, rows, inputs)
+    for tile in range(count):
+        holder[tile] = lax.fori_loop(
+            0, count,
+            lambda k, found: found + jnp.where(owned[k] == tile, rank_of(k, nz, ny), 0),
+            jnp.int32(0),
+        )
+    scale = 0.5 / jnp.maximum(length * pairs[owned[me]], 1.0)
+    direct = jnp.concatenate([kept[holder[tile]] for tile in range(count)], axis=0).T
+    each = 128 // rows
+    lane = lax.broadcasted_iota(jnp.int32, (rows, 128), 1) // rows
+    mirror = [[None] * (count // each) for _ in range(chans)]
+    for tile in range(count):
+        block = mirrored[holder[tile]]
+        if chans * rows < 128:
+            block = jnp.concatenate([block, jnp.zeros((rows, 128 - chans * rows), block.dtype)], axis=1)
+        place = tile % each
+        for ch in range(chans):
+            group, offset = divmod(ch * rows, 128)
+            piece = block[:, group * 128 : (group + 1) * 128]
+            turn = (place * rows - offset) % 128
+            if turn:
+                piece = pltpu.roll(piece, turn, 1)
+            held = mirror[ch][tile // each]
+            mirror[ch][tile // each] = piece if held is None else jnp.where(lane == place, piece, held)
+    for ch in range(chans):
+        left = direct[ch * rows : (ch + 1) * rows]
+        right = jnp.concatenate(mirror[ch], axis=1)
+        out[:, ch, 0, :] = (left + right) * scale
+        out[:, ch, 1, :] = (left - right) * scale
 
 
 def shards(nz, ny, voltages, antenna_flags, owned_tile):
     count = nz * ny * CORES
-    me = lax.axis_index("tm")
     chans, _, inputs, samples = voltages.shape
     rows = inputs // count
-    sub_length = samples // antenna_flags.shape[0]
     first = chans // 4 if ny > 1 else 0
     held = jnp.bfloat16 if rows % 16 == 0 else jnp.float32
     vmem = pl.BlockSpec(memory_space=pltpu.VMEM)
     smem = pl.BlockSpec(memory_space=pltpu.SMEM)
     dma = pltpu.SemaphoreType.DMA
-    summed, mirrored = pl.pallas_call(
+    sizes = antenna_flags.shape
+    padded = jnp.pad(antenna_flags, ((0, -sizes[0] % 8), (0, -sizes[1] % 128)))
+    length = samples // sizes[0]
+    blocks = jax.ShapeDtypeStruct((count, rows, chans * rows), jnp.float32)
+    kept, mirrored, words = pl.pallas_call(
         functools.partial(kernel, nz, ny, first),
-        out_shape=(
-            jax.ShapeDtypeStruct((chans, rows, inputs), jnp.float32),
-            jax.ShapeDtypeStruct((count, rows, chans * rows), jnp.float32),
-        ),
-        in_specs=[smem, smem, vmem],
-        out_specs=(vmem, vmem),
+        out_shape=(blocks, blocks, jax.ShapeDtypeStruct((count * sizes[0], sizes[1]), jnp.int32)),
+        in_specs=[smem, smem, vmem, vmem],
+        out_specs=(vmem, vmem, vmem),
         scratch_shapes=[
             pltpu.VMEM((count, rows, samples), held),
             pltpu.VMEM((inputs, 2 * samples), held),
@@ -228,33 +288,27 @@
             pltpu.VMEM((chans, ny, nz, rows, inputs), jnp.float32),
             pltpu.VMEM((chans, nz, rows, inputs), jnp.float32),
             pltpu.VMEM((chans, nz - 1, ny, rows, inputs), jnp.float32),
+            pltpu.VMEM((chans, rows, inputs), jnp.float32),
             pltpu.VMEM((count, rows, chans * rows), jnp.float32),
+            pltpu.VMEM((count,) + padded.shape, jnp.int32),
             dma((chans,)), dma((chans,)), dma((chans,)), dma((chans,)),
             dma((chans, nz - 1)), dma((chans, nz - 1)), dma((count,)), dma((count,)),
+            dma((count,)), dma((count,)),
         ],
         compiler_params=pltpu.CompilerParams(
             collective_id=0, has_side_effects=True, vmem_limit_bytes=60 * 1024 * 1024
         ),
-    )(owned_tile, antenna_flags, voltages.reshape(chans, 2, count, rows, samples))
-
-    words = lax.all_gather(antenna_flags, "tm", axis=0, tiled=True)
-    shifts = jnp.arange(32, dtype=jnp.int32)
-    bits = jnp.bitwise_and(jnp.right_shift(words[:, :, None], shifts), 1)
-    good = jnp.broadcast_to(bits[..., None], bits.shape + (2,)).reshape(words.shape[0], count, rows)
-    good = good.astype(jnp.bfloat16)
-    own = lax.dynamic_index_in_dim(good, owned_tile[me], 1, False)
-    counts = jnp.einsum("su,stj->utj", own, good, preferred_element_type=jnp.float32)
-    scale = 0.5 / jnp.maximum(sub_length * counts, 1.0)
-
-    holder = jnp.zeros((count,), jnp.int32).at[owned_tile].set(
-        rank_of(jnp.arange(count, dtype=jnp.int32), nz, ny)
-    )
-    direct = summed.reshape(chans, rows, count, rows)[:, :, holder].transpose(1, 0, 2, 3)
-    mirror = mirrored.reshape(count, rows, chans, rows)[holder].transpose(1, 2, 0, 3)
-    scale = scale[:, None]
-    real = ((direct + mirror) * scale).reshape(rows, chans, inputs)
-    imag = ((direct - mirror) * scale).reshape(rows, chans, inputs)
-    return jnp.stack([real, imag], axis=2)
+    )(owned_tile, antenna_flags, padded, voltages.reshape(chans, 2, count, rows, samples))
+    return pl.pallas_call(
+        functools.partial(assemble, nz, ny, length),
+        out_shape=jax.ShapeDtypeStruct((rows, chans, 2, inputs), jnp.float32),
+        in_specs=[smem, vmem, vmem, vmem],
+        out_specs=vmem,
+        scratch_shapes=[
+            pltpu.VMEM((count, rows, inputs), jnp.float32),
+            pltpu.SMEM((count,), jnp.int32),
+        ],
+    )(owned_tile, words, kept, mirrored)
 
 
 def solution(mesh):

time: 126 us -> 86.5 us (0.69)
  blocking collectives: 23.2 us -> 0 us
  local copies, waits for them, and re-layouts: 18.5 us -> 1.27 us
  Pallas kernels: 76.7 us -> 84.8 us
  other arithmetic: 4.58 us -> 0 us
  between operations: 2.06 us -> 0.01 us
    all_gather x1 -> x0, blocking collectives: 23.2 us -> none  [shards(): words = lax.all_gather(antenna_flags, 'tm', axis=0, tiled=True)]
    pallas_call x1 -> x2, Pallas kernels: 76.7 us -> 84.8 us  [the longest x1 77 us: shards(): pl.pallas_call(functools.partial(kernel, nz, ny, first), out_shape=(block...]
    gather x2 -> x0, local copies, waits for them, and re-layouts: 5.64 us -> none  [the longest x1 3.66 us: shards(): summed.reshape(chans, rows, count, rows)[:, :, holder].transpose(1, 0, 2, 3)]
    mul x1 -> x0, other arithmetic: 4.47 us -> none  [shards(): real = ((direct + mirror) * scale).reshape(rows, chans, inputs)]
    reshape x3 -> x0, local copies, waits for them, and re-layouts: 4.05 us -> none  [the longest x2 3.58 us: shards(): summed.reshape(chans, rows, count, rows)[:, :, holder].transpose(1, 0, 2, 3)]
    mul x2 -> x0, local copies, waits for them, and re-layouts: 4.03 us -> none  [the longest x1 2.81 us: shards(): real = ((direct + mirror) * scale).reshape(rows, chans, inputs)]
    another operation x3 -> x0, local copies, waits for them, and re-layouts: 3.44 us -> none  [shards(): return jnp.stack([real, imag], axis=2)]
    pad x0 -> x1, local copies, waits for them, and re-layouts: none -> 1.27 us  [shards(): padded = jnp.pad(antenna_flags, ((0, -sizes[0] % 8), (0, -sizes[1] % 128)))]
where the time goes in v2:
time: 86.5 us; the launch traced here: 86.1 us
  Pallas kernels  84.8 us (98%)
  local copies, waits for them, and re-layouts  1.27 us (1%)
    pallas_call x1, Pallas kernels, shards(): pl.pallas_call(functools.partial(kernel, nz, ny, first), out_shape=(block...  77 us
    pallas_call x1, Pallas kernels, shards(): pl.pallas_call(functools.partial(assemble, nz, ny, length), out_shape=jax...  7.78 us

profile of v2, /device:TPU:0, one launch (start us, length us, event | category | flops | bytes accessed | tf_op | source)
XLA Modules:
  0.0 86.1 jit_solution(17333944312904359859)
XLA Ops:
  0.0 1.3 %pad.4.packed = s32[8,128]{1,0:T(8,128)} pad(s32[2,8]{1,0:T(2,128)} %flags.1, s32[]{:T(128)} %constant.0.clone.1), padding=0_6x0_120 | pad | bytes 4164 | tf_op jit(solution)/shard_map/jit(_pad)/pad | solution.py:276
  1.3 77.0 %shard_map.37 = (f32[16,32,256]{2,1,0:T(8,128)}, f32[16,32,256]{2,1,0:T(8,128)}, s32[32,8]{1,0:T(8,128)}) custom-call(s32[16]{0:T(128)} %owned.3, s32[2,8]{1,0:T(2,128)} %flags.1, s32[8,128]{1,0:T(8,128)} %pad.4.packed, bf16[8,2,16,32,256]{4,3,2,1,0:T(8,128)(2,1)} %bitcast.1), custom_call_target="tpu_custom_call" | custom-call | tf_op jit(solution)/shard_map/pallas_call | solution.py:279
  78.3 7.8 %shard_map.38 = f32[32,8,2,512]{3,2,1,0:T(2,128)} custom-call(s32[16]{0:T(128)} %owned.3, s32[32,8]{1,0:T(8,128)} %get-tuple-element.8.words_all, f32[16,32,256]{2,1,0:T(8,128)} %get-tuple-element.9.kept, f32[16,32,256]{2,1,0:T(8,128)} %get-tuple-element.10.mirrored), custom_call_target="tpu_custom_call" | custom-call | tf_op jit(solution)/shard_map/pallas_call | solution.py:302

commit v3 on v2

--- a/solution.py
+++ b/solution.py
@@ -106,13 +106,14 @@
                 plane[tile * rows : (tile + 1) * rows, part * samples : (part + 1) * samples] = value
         half = inputs // CORES
         pair = plane[...].astype(jnp.bfloat16)
+        pair = jnp.concatenate([pair, pair], axis=1)
         for turn in range(CORES):
             c = (core + 1 + turn) % CORES
             part = plane[pl.ds(pl.multiple_of(c * half, half), half), :].astype(jnp.bfloat16)
             other = jnp.concatenate([part[:, samples:], -part[:, :samples]], axis=1)
             dims = (((1,), (1,)), ((), ()))
-            total = lax.dot_general(part, pair, dims, preferred_element_type=jnp.float32)
-            total += lax.dot_general(other, pair, dims, preferred_element_type=jnp.float32)
+            left = jnp.concatenate([part, other], axis=1)
+            total = lax.dot_general(left, pair, dims, preferred_element_type=jnp.float32)
             gram[ch, c] = total.reshape(ny, nz, rows, inputs)
             if turn == 0:
                 core_copy(ch).start()
@@ -127,11 +128,13 @@
             z_copy(ch, 0, False).start()
             return
 
-        @pl.when(ch < first)
+        wide = jnp.logical_and(ch >= 1, ch < 1 + first)
+
+        @pl.when(wide)
         def _():
             z_copy(ch, 0, True).start()
 
-        @pl.when(ch >= first)
+        @pl.when(jnp.logical_not(wide))
         def _():
             y_copy(ch).start()
 
@@ -179,44 +182,60 @@
         y_last_copy(ch).wait()
         summed[ch] = from_z[ch, nz - 2, y] + from_y[ch, 0]
 
+    groups = turned.shape[0]
+    size = chans // groups
+    mine = rank_of(me, nz, ny)
+
+    def block_copy(group, step):
+        target = lax.rem(me + step, count)
+        return remote(
+            turned.at[group, rank_of(target, nz, ny)], mirrored.at[group, mine],
+            fs.at[group, step], fr.at[group, step], target,
+        )
+
+    def exchange(group):
+        value = summed[group * size : (group + 1) * size].reshape(size * rows, inputs)
+        value = value.T.reshape(count, rows, size * rows)
+        turned[group] = value
+        kept[group] = value
+        for step in range(1, count):
+            block_copy(group, step).start()
+
     events = []
+    ends = [0.0] * groups
+    start = 0.0
     for ch in range(chans):
+        mark = len(events)
         if ny == 1:
             for step in range(nz - 1):
                 events.append((step * chans + ch, after_z, (ch, step, False)))
-        elif ch < first:
+        elif 1 <= ch < 1 + first:
             for step in range(nz - 1):
                 events.append((8.0 * (step + 1), after_z, (ch, step, True)))
             events.append((8.0 * nz, after_last_y, (ch,)))
         else:
-            start = 5.8 * (ch - first + 1)
+            start += 5.8
             events.append((start, after_y, (ch,)))
             for step in range(nz - 1):
                 events.append((start + 4.6 * (step + 1), after_z, (ch, step, False)))
+        last = max(event[0] for event in events[mark:])
+        ends[ch // size] = max(ends[ch // size], last + 0.01)
+    for group in range(groups):
+        events.append((ends[group], exchange, (group,)))
     for _, act, args in sorted(events, key=lambda event: event[0]):
         act(*args)
-
-    flipped = summed[...].reshape(chans * rows, inputs).T.reshape(count, rows, chans * rows)
-    turned[...] = flipped
-    kept[...] = flipped
-    mine = rank_of(me, nz, ny)
-
-    def block_copy(step):
-        target = lax.rem(me + step, count)
-        return remote(turned.at[rank_of(target, nz, ny)], mirrored.at[mine], fs.at[step], fr.at[step], target)
-
-    for step in range(1, count):
-        block_copy(step).start()
-    for step in range(1, count):
-        block_copy(step).wait()
-    mirrored[mine] = turned[mine]
+    for group in range(groups):
+        for step in range(1, count):
+            block_copy(group, step).wait()
+        mirrored[group, mine] = turned[group, mine]
 
 
 def assemble(nz, ny, length, owned, words_all, kept, mirrored, out, pairs, holder):
-    count, rows, width = kept.shape
+    groups, count, rows, width = kept.shape
     slots, words = words_all.shape
     inputs = count * rows
-    chans = width // rows
+    chans = groups * width // rows
+    size = chans // groups
     span = inputs // words
     me = lax.axis_index("tm")
     every = words_all[...]
@@ -239,28 +258,26 @@
             jnp.int32(0),
         )
     scale = 0.5 / jnp.maximum(length * pairs[owned[me]], 1.0)
-    direct = jnp.concatenate([kept[holder[tile]] for tile in range(count)], axis=0).T
     each = 128 // rows
     lane = lax.broadcasted_iota(jnp.int32, (rows, 128), 1) // rows
-    mirror = [[None] * (count // each) for _ in range(chans)]
-    for tile in range(count):
-        block = mirrored[holder[tile]]
-        if chans * rows < 128:
-            block = jnp.concatenate([block, jnp.zeros((rows, 128 - chans * rows), block.dtype)], axis=1)
-        place = tile % each
-        for ch in range(chans):
-            group, offset = divmod(ch * rows, 128)
-            piece = block[:, group * 128 : (group + 1) * 128]
-            turn = (place * rows - offset) % 128
-            if turn:
-                piece = pltpu.roll(piece, turn, 1)
-            held = mirror[ch][tile // each]
-            mirror[ch][tile // each] = piece if held is None else jnp.where(lane == place, piece, held)
-    for ch in range(chans):
-        left = direct[ch * rows : (ch + 1) * rows]
-        right = jnp.concatenate(mirror[ch], axis=1)
-        out[:, ch, 0, :] = (left + right) * scale
-        out[:, ch, 1, :] = (left - right) * scale
+    for group in range(groups):
+        direct = jnp.concatenate([kept[group, holder[tile]] for tile in range(count)], axis=0).T
+        mirror = [[None] * (count // each) for _ in range(size)]
+        for tile in range(count):
+            piece = mirrored[group, holder[tile]]
+            if size * rows < 128:
+                piece = jnp.concatenate([piece, jnp.zeros((rows, 128 - size * rows), piece.dtype)], axis=1)
+            place = tile % each
+            for ch in range(size):
+                turn = (place - ch) * rows % 128
+                moved = pltpu.roll(piece, turn, 1) if turn else piece
+                held = mirror[ch][tile // each]
+                mirror[ch][tile // each] = moved if held is None else jnp.where(lane == place, moved, held)
+        for ch in range(size):
+            left = direct[ch * rows : (ch + 1) * rows]
+            right = jnp.concatenate(mirror[ch], axis=1)
+            out[:, group * size + ch, 0, :] = (left + right) * scale
+            out[:, group * size + ch, 1, :] = (left - right) * scale
 
 
 def shards(nz, ny, voltages, antenna_flags, owned_tile):
@@ -275,7 +292,9 @@
     sizes = antenna_flags.shape
     padded = jnp.pad(antenna_flags, ((0, -sizes[0] % 8), (0, -sizes[1] % 128)))
     length = samples // sizes[0]
-    blocks = jax.ShapeDtypeStruct((count, rows, chans * rows), jnp.float32)
+    groups = max(1, chans * rows // 128)
+    shape = (groups, count, rows, chans // groups * rows)
+    blocks = jax.ShapeDtypeStruct(shape, jnp.float32)
     kept, mirrored, words = pl.pallas_call(
         functools.partial(kernel, nz, ny, first),
         out_shape=(blocks, blocks, jax.ShapeDtypeStruct((count * sizes[0], sizes[1]), jnp.int32)),
@@ -289,10 +308,10 @@
             pltpu.VMEM((chans, nz, rows, inputs), jnp.float32),
             pltpu.VMEM((chans, nz - 1, ny, rows, inputs), jnp.float32),
             pltpu.VMEM((chans, rows, inputs), jnp.float32),
-            pltpu.VMEM((count, rows, chans * rows), jnp.float32),
+            pltpu.VMEM(shape, jnp.float32),
             pltpu.VMEM((count,) + padded.shape, jnp.int32),
             dma((chans,)), dma((chans,)), dma((chans,)), dma((chans,)),
-            dma((chans, nz - 1)), dma((chans, nz - 1)), dma((count,)), dma((count,)),
+            dma((chans, nz - 1)), dma((chans, nz - 1)), dma((groups, count)), dma((groups, count)),
             dma((count,)), dma((count,)),
         ],
         compiler_params=pltpu.CompilerParams(

time: 86.5 us -> 86.4 us (level)
  no operation moved by 1% of the time
where the time goes in v3:
time: 86.4 us; the launch traced here: 86.3 us
  Pallas kernels  85 us (98%)
  local copies, waits for them, and re-layouts  1.27 us (1%)
    pallas_call x1, Pallas kernels, shards(): pl.pallas_call(functools.partial(kernel, nz, ny, first), out_shape=(block...  77.3 us
    pallas_call x1, Pallas kernels, shards(): pl.pallas_call(functools.partial(assemble, nz, ny, length), out_shape=jax...  7.71 us

profile of v3, /device:TPU:0, one launch (start us, length us, event | category | flops | bytes accessed | tf_op | source)
XLA Modules:
  0.0 86.3 jit_solution(8938347828291420039)
XLA Ops:
  0.0 1.3 %pad.4.packed = s32[8,128]{1,0:T(8,128)} pad(s32[2,8]{1,0:T(2,128)} %flags.1, s32[]{:T(128)} %constant.0.clone.1), padding=0_6x0_120 | pad | bytes 4164 | tf_op jit(solution)/shard_map/jit(_pad)/pad | solution.py:293
  1.3 77.3 %shard_map.37 = (f32[2,16,32,128]{3,2,1,0:T(8,128)}, f32[2,16,32,128]{3,2,1,0:T(8,128)}, s32[32,8]{1,0:T(8,128)}) custom-call(s32[16]{0:T(128)} %owned.3, s32[2,8]{1,0:T(2,128)} %flags.1, s32[8,128]{1,0:T(8,128)} %pad.4.packed, bf16[8,2,16,32,256]{4,3,2,1,0:T(8,128)(2,1)} %bitcast.1), custom_call_target="tpu_custom_call" | custom-call | tf_op jit(solution)/shard_map/pallas_call | solution.py:298
  78.5 7.7 %shard_map.38 = f32[32,8,2,512]{3,2,1,0:T(2,128)} custom-call(s32[16]{0:T(128)} %owned.3, s32[32,8]{1,0:T(8,128)} %get-tuple-element.8.words_all, f32[2,16,32,128]{3,2,1,0:T(8,128)} %get-tuple-element.9.kept, f32[2,16,32,128]{3,2,1,0:T(8,128)} %get-tuple-element.10.mirrored), custom_call_target="tpu_custom_call" | custom-call | tf_op jit(solution)/shard_map/pallas_call | solution.py:321

commit v4 on v3

--- a/solution.py
+++ b/solution.py
@@ -217,7 +217,7 @@
             start += 5.8
             events.append((start, after_y, (ch,)))
             for step in range(nz - 1):
-                events.append((start + 4.6 * (step + 1), after_z, (ch, step, False)))
+                events.append((start + 3.8 * (step + 1), after_z, (ch, step, False)))
         last = max(event[0] for event in events[mark:])
         ends[ch // size] = max(ends[ch // size], last + 0.01)
     for group in range(groups):
@@ -290,7 +290,6 @@
     smem = pl.BlockSpec(memory_space=pltpu.SMEM)
     dma = pltpu.SemaphoreType.DMA
     sizes = antenna_flags.shape
-    padded = jnp.pad(antenna_flags, ((0, -sizes[0] % 8), (0, -sizes[1] % 128)))
     length = samples // sizes[0]
     groups = max(1, chans * rows // 128)
     shape = (groups, count, rows, chans // groups * rows)
@@ -309,7 +308,7 @@
             pltpu.VMEM((chans, nz - 1, ny, rows, inputs), jnp.float32),
             pltpu.VMEM((chans, rows, inputs), jnp.float32),
             pltpu.VMEM(shape, jnp.float32),
-            pltpu.VMEM((count,) + padded.shape, jnp.int32),
+            pltpu.VMEM((count,) + sizes, jnp.int32),
             dma((chans,)), dma((chans,)), dma((chans,)), dma((chans,)),
             dma((chans, nz - 1)), dma((chans, nz - 1)), dma((groups, count)), dma((groups, count)),
             dma((count,)), dma((count,)),
@@ -317,7 +316,7 @@
         compiler_params=pltpu.CompilerParams(
             collective_id=0, has_side_effects=True, vmem_limit_bytes=60 * 1024 * 1024
         ),
-    )(owned_tile, antenna_flags, padded, voltages.reshape(chans, 2, count, rows, samples))
+    )(owned_tile, antenna_flags, antenna_flags, voltages.reshape(chans, 2, count, rows, samples))
     return pl.pallas_call(
         functools.partial(assemble, nz, ny, length),
         out_shape=jax.ShapeDtypeStruct((rows, chans, 2, inputs), jnp.float32),

time: 86.4 us -> 85.5 us (0.990)
  local copies, waits for them, and re-layouts: 1.27 us -> 0 us
    pad x1 -> x0, local copies, waits for them, and re-layouts: 1.27 us -> none  [shards(): padded = jnp.pad(antenna_flags, ((0, -sizes[0] % 8), (0, -sizes[1] % 128)))]
where the time goes in v4:
time: 85.5 us; the launch traced here: 85.4 us
  Pallas kernels  85.4 us (100%)
    pallas_call x1, Pallas kernels, shards(): pl.pallas_call(functools.partial(kernel, nz, ny, first), out_shape=(block...  77.7 us
    pallas_call x1, Pallas kernels, shards(): pl.pallas_call(functools.partial(assemble, nz, ny, length), out_shape=jax...  7.7 us

profile of v4, /device:TPU:0, one launch (start us, length us, event | category | flops | bytes accessed | tf_op | source)
XLA Modules:
  0.0 85.4 jit_solution(2436936561834125283)
XLA Ops:
  0.0 77.7 %shard_map.37 = (f32[2,16,32,128]{3,2,1,0:T(8,128)}, f32[2,16,32,128]{3,2,1,0:T(8,128)}, s32[32,8]{1,0:T(8,128)}) custom-call(s32[16]{0:T(128)} %owned.3, s32[2,8]{1,0:T(2,128)} %packed.1, s32[2,8]{1,0:T(2,128)} %packed.1, bf16[8,2,16,32,256]{4,3,2,1,0:T(8,128)(2,1)} %bitcast.1), custom_call_target="tpu_custom_call" | custom-call | tf_op jit(solution)/shard_map/pallas_call | solution.py:297
  77.7 7.7 %shard_map.38 = f32[32,8,2,512]{3,2,1,0:T(2,128)} custom-call(s32[16]{0:T(128)} %owned.3, s32[32,8]{1,0:T(8,128)} %get-tuple-element.8.words_all, f32[2,16,32,128]{3,2,1,0:T(8,128)} %get-tuple-element.9.kept, f32[2,16,32,128]{3,2,1,0:T(8,128)} %get-tuple-element.10.mirrored), custom_call_target="tpu_custom_call" | custom-call | tf_op jit(solution)/shard_map/pallas_call | solution.py:320
